TPU v7x, 32 devices: a whole 2x2x4 slice. The times are simulated.
32 devices in a mesh: dp: 32 (over z, y, x, core).
Axes of the slice: x: 2, y: 2, z: 4, core: 2. Of those that a mesh axis runs over, the one named last changes fastest.
Arguments:
- grads: float32 [32, 163840], P('dp'), may hold values from -6 to 6
- master: float32 [163840], P('dp')
- moment1: float32 [163840], P('dp'), may hold values from -4 to 4
- moment2: float32 [163840], P('dp'), may hold values from 0.1 to 2
- tensor_rows: int32 [8], replicated, may hold values from 1 to 16, 32 in all
- step_count: int32 [1], replicated, may hold values from 1 to 19
Outputs:
- new_weights: bfloat16 [163840], replicated
- new_master: float32 [163840], P('dp')
- new_moment1: float32 [163840], P('dp')
- new_moment2: float32 [163840], P('dp')
All inputs are finite; a program needn't handle non-finite values.
Results may differ from a plain program's by a relative error of at most 0.001.
Values may be sent and summed in bfloat16 or wider, within the bound.
A program may use at most 64 MiB of HBM per device.

v0:
```python
import jax
import jax.numpy as jnp
from jax import lax
from jax.sharding import PartitionSpec as P

D = 5120


def swapped(value, axis, bit):
    mask = 2**bit
    pairs = [(source, source ^ mask) for source in range(lax.axis_size(axis))]
    return lax.ppermute(value, axis, pairs)


def tensor_sums(values, onehot, row_count, width):
    rows = values.reshape(row_count, width)
    row_sums = jnp.sum(rows * rows, axis=1)
    return jnp.sum(onehot * row_sums[:, None], axis=0)


def body(grads, master, moment1, moment2, tensor_rows, step_count):
    count = lax.axis_size("dp")
    me = lax.axis_index("dp")
    owned = master.shape[0]
    width = D
    row_count = owned // width
    ends = jnp.cumsum(tensor_rows)
    starts = ends - tensor_rows
    row_index = me * row_count + jnp.arange(row_count, dtype=jnp.int32)
    onehot = (
        (row_index[:, None] >= starts[None, :]) & (row_index[:, None] < ends[None, :])
    ).astype(jnp.float32)
    local_wsq = tensor_sums(master, onehot, row_count, width)
    flat = grads[0]
    buffer = flat
    for bit in reversed(range(count.bit_length() - 1)):
        halves = buffer.reshape(2, -1)
        upper = me // 2**bit % 2 == 1
        keep = jnp.where(upper, halves[1], halves[0])
        give = jnp.where(upper, halves[0], halves[1])
        buffer = keep + swapped(give.astype(jnp.bfloat16), "dp", bit).astype(give.dtype)
    grad = buffer / jnp.float32(count)
    new_moment1 = 0.9 * moment1 + 0.1 * grad
    new_moment2 = 0.999 * moment2 + 0.001 * grad * grad
    steps = step_count[0].astype(jnp.float32)
    first = new_moment1 / (1.0 - jnp.power(jnp.float32(0.9), steps))
    second = new_moment2 / (1.0 - jnp.power(jnp.float32(0.999), steps))
    update = first / (jnp.sqrt(second) + 1e-06) + 0.1 * master
    local_usq = tensor_sums(update, onehot, row_count, width)
    wsq, usq = lax.psum((local_wsq, local_usq), "dp")
    ratio = jnp.sqrt(wsq / (usq + 1e-06))
    row_ratio = jnp.sum(onehot * ratio[None, :], axis=1)
    new_master = (
        master.reshape(row_count, width)
        - 0.2 * row_ratio[:, None] * update.reshape(row_count, width)
    ).reshape(owned)
    new_weights = lax.all_gather(new_master.astype(jnp.bfloat16), "dp", axis=0, tiled=True)
    return (new_weights, new_master, new_moment1, new_moment2)


def solution(mesh):
    placed = (P("dp", None), P("dp"), P("dp"), P("dp"), P(), P())
    return jax.shard_map(
        body,
        mesh=mesh,
        in_specs=placed,
        out_specs=(P(), P("dp"), P("dp"), P("dp")),
        check_vma=False,
    )
```

profile of v0, /device:TPU:1, one launch (start us, length us, event | category | flops | bytes accessed | tf_op | source)
XLA Modules:
  0.0 115.3 jit_solution(14798427415368217003)
XLA Ops:
  0.7 2.2 %fusion.1 = bf16[81920]{0:T(1024)(128)(2,1)S(1)} fusion(pred[]{:T(512)S(6)} %eq.25, f32[1,163840]{1,0:T(1,128)} %param.6), kind=kLoop, calls=%fused_computation.3 | loop fusion | flops 81920 | bytes 491521 | tf_op jit(solution)/shard_map/convert_element_type | solution.py:41
  2.8 3.2 %collective-permute-start = (bf16[81920]{0:T(1024)(128)(2,1)S(1)}, bf16[81920]{0:T(1024)(128)(2,1)S(1)}, u32[]{:S(2)}, u32[]{:S(2)}) collective-permute-start(bf16[81920]{0:T(1024)(128)(2,1)S(1)} %fusion.1), channel_id=1, source_target_pairs={{0,16},{1,17},{2,18},{3,19},{4,20},{5,21},{6,22},{7,23},{8,24},{9,... | collective-permute-start | bytes 491528 | tf_op jit(solution)/shard_map/ppermute | solution.py:12
  6.0 0.3 broadcast_select_fusion.1
  6.4 7.0 %collective-permute-done = bf16[81920]{0:T(1024)(128)(2,1)S(1)} collective-permute-done((bf16[81920]{0:T(1024)(128)(2,1)S(1)}, bf16[81920]{0:T(1024)(128)(2,1)S(1)}, u32[]{:S(2)}, u32[]{:S(2)}) %collective-permute-start) | collective-permute-done | bytes 163872 | tf_op jit(solution)/shard_map/ppermute | solution.py:12
  13.5 1.3 %collective-permute-start.1 = (bf16[40960]{0:T(1024)(128)(2,1)S(1)}, bf16[40960]{0:T(1024)(128)(2,1)S(1)}, u32[]{:S(2)}, u32[]{:S(2)}) collective-permute-start(bf16[40960]{0:T(1024)(128)(2,1)S(1)} %select_convert_fusion), channel_id=1, source_target_pairs={{0,8},{1,9},{2,10},{3,11},{4,12},{5,13},{6,14},{7,15},{8,0},{9,1},... | collective-permute-start | bytes 245768 | tf_op jit(solution)/shard_map/ppermute | solution.py:12
  14.8 2.1 %collective-permute-done.1 = bf16[40960]{0:T(1024)(128)(2,1)S(1)} collective-permute-done((bf16[40960]{0:T(1024)(128)(2,1)S(1)}, bf16[40960]{0:T(1024)(128)(2,1)S(1)}, u32[]{:S(2)}, u32[]{:S(2)}) %collective-permute-start.1) | collective-permute-done | bytes 81952 | tf_op jit(solution)/shard_map/ppermute | solution.py:12
  16.9 1.1 collective-permute-start.2
  18.0 1.8 %collective-permute-done.2 = bf16[20480]{0:T(1024)(128)(2,1)S(1)} collective-permute-done((bf16[20480]{0:T(1024)(128)(2,1)S(1)}, bf16[20480]{0:T(1024)(128)(2,1)S(1)}, u32[]{:S(2)}, u32[]{:S(2)}) %collective-permute-start.2) | collective-permute-done | bytes 40992 | tf_op jit(solution)/shard_map/ppermute | solution.py:12
  19.9 1.1 collective-permute-start.3
  20.9 1.9 %collective-permute-done.3 = bf16[10240]{0:T(1024)(128)(2,1)S(1)} collective-permute-done((bf16[10240]{0:T(1024)(128)(2,1)S(1)}, bf16[10240]{0:T(1024)(128)(2,1)S(1)}, u32[]{:S(2)}, u32[]{:S(2)}) %collective-permute-start.3) | collective-permute-done | bytes 20512 | tf_op jit(solution)/shard_map/ppermute | solution.py:12
  22.9 0.0 copy-start.1
  22.9 0.0 copy-start.2
  22.9 4.5 %collective-permute-start.4 = (bf16[5120]{0:T(1024)(128)(2,1)S(1)}, bf16[5120]{0:T(1024)(128)(2,1)S(1)}, u32[]{:S(2)}, u32[]{:S(2)}) collective-permute-start(bf16[5120]{0:T(1024)(128)(2,1)S(1)} %select_convert_fusion.3), channel_id=1, source_target_pairs={{0,1},{1,0},{2,3},{3,2},{4,5},{5,4},{6,7},{7,6},{8,9},{9,8},{10,11... | collective-permute-start | bytes 30728 | tf_op jit(solution)/shard_map/ppermute | solution.py:12
  28.1 0.0 copy-start.4
  28.1 0.6 copy-done.4
  28.8 0.2 reduce-window.8
  29.0 1.3 %multiply_reduce_fusion = (f32[]{:T(128)}, f32[5120]{0:T(1024)S(1)}, f32[5120]{0:T(1024)}, f32[5120]{0:T(1024)}, f32[]{:T(128)}) fusion(f32[5120]{0:T(1024)S(1)} %copy-done.1, f32[]{:T(128)} %bitcast.4, f32[]{:T(128)} %bitcast.3, bf16[5120]{0:T(1024)(128)(2,1)S(1)} %collective-permute-done.4, f32[10240]{0:T(1024)S(1)} %convert_add_fusion.3, pred[]{:T(512)S(6)} %eq.21, ...), kind=kLoop, calls=%fused_computation.12 | loop fusion | flops 107518 | bytes 174097 | tf_op jit(solution)/shard_map/reduce_sum | solution.py:17
  30.3 0.7 broadcast_select_fusion.2
  31.0 0.6 broadcast_select_fusion.3
  31.5 38.7 %all-reduce = (f32[8]{0:T(128)S(1)}, f32[8]{0:T(128)S(1)}) all-reduce(f32[8]{0:T(128)S(1)} %broadcast_select_fusion.3, f32[8]{0:T(128)S(1)} %get-tuple-element.8), channel_id=1, replica_groups=mesh['dp'=32] {'dp'}, use_global_device_ids=true, to_apply=%region_2.3 | all-reduce | flops 16 | bytes 128 | tf_op jit(solution)/shard_map/psum | solution.py:50
  70.2 0.6 select_reduce_fusion
  71.5 0.6 fusion.2
  72.1 42.4 %all_gather.3 = bf16[163840]{0:T(1024)(128)(2,1)S(1)} all-gather(bf16[5120]{0:T(1024)(128)(2,1)S(1)} %get-tuple-element.6), channel_id=1, replica_groups=mesh['dp'=32] {'dp'}, dimensions={0}, use_global_device_ids=true | all-gather | bytes 337920 | tf_op jit(solution)/shard_map/all_gather | solution.py:57
  114.5 0.7 copy.12
  (15 shorter events, 0.1 us)
Async XLA Ops:
  0.6 5.4 %copy-start = (f32[1,163840]{1,0:T(1,128)S(1)}, f32[1,163840]{1,0:T(1,128)}, u32[]{:S(2)}) copy-start(f32[1,163840]{1,0:T(1,128)} %param.6) | copy-start | bytes 1966084
  2.8 10.6 %collective-permute-start = (bf16[81920]{0:T(1024)(128)(2,1)S(1)}, bf16[81920]{0:T(1024)(128)(2,1)S(1)}, u32[]{:S(2)}, u32[]{:S(2)}) collective-permute-start(bf16[81920]{0:T(1024)(128)(2,1)S(1)} %fusion.1), channel_id=1, source_target_pairs={{0,16},{1,17},{2,18},{3,19},{4,20},{5,21},{6,22},{7,23},{8,24},{9,... | collective-permute-start | bytes 491528 | tf_op jit(solution)/shard_map/ppermute | solution.py:12
  13.5 3.4 %collective-permute-start.1 = (bf16[40960]{0:T(1024)(128)(2,1)S(1)}, bf16[40960]{0:T(1024)(128)(2,1)S(1)}, u32[]{:S(2)}, u32[]{:S(2)}) collective-permute-start(bf16[40960]{0:T(1024)(128)(2,1)S(1)} %select_convert_fusion), channel_id=1, source_target_pairs={{0,8},{1,9},{2,10},{3,11},{4,12},{5,13},{6,14},{7,15},{8,0},{9,1},... | collective-permute-start | bytes 245768 | tf_op jit(solution)/shard_map/ppermute | solution.py:12
  16.9 2.9 %collective-permute-start.2 = (bf16[20480]{0:T(1024)(128)(2,1)S(1)}, bf16[20480]{0:T(1024)(128)(2,1)S(1)}, u32[]{:S(2)}, u32[]{:S(2)}) collective-permute-start(bf16[20480]{0:T(1024)(128)(2,1)S(1)} %select_convert_fusion.1), channel_id=1, source_target_pairs={{0,4},{1,5},{2,6},{3,7},{4,0},{5,1},{6,2},{7,3},{8,12},{9,13},{10,... | collective-permute-start | bytes 122888 | tf_op jit(solution)/shard_map/ppermute | solution.py:12
  19.9 3.0 %collective-permute-start.3 = (bf16[10240]{0:T(1024)(128)(2,1)S(1)}, bf16[10240]{0:T(1024)(128)(2,1)S(1)}, u32[]{:S(2)}, u32[]{:S(2)}) collective-permute-start(bf16[10240]{0:T(1024)(128)(2,1)S(1)} %select_convert_fusion.2), channel_id=1, source_target_pairs={{0,2},{1,3},{2,0},{3,1},{4,6},{5,7},{6,4},{7,5},{8,10},{9,11},{10,... | collective-permute-start | bytes 61448 | tf_op jit(solution)/shard_map/ppermute | solution.py:12
  22.8 6.1 %copy-start.3 = (f32[5120]{0:T(1024)S(1)}, f32[5120]{0:T(1024)}, u32[]{:S(2)}) copy-start(f32[5120]{0:T(1024)} %param.8) | copy-start | bytes 61444
  22.9 6.1 %copy-start.1 = (f32[5120]{0:T(1024)S(1)}, f32[5120]{0:T(1024)}, u32[]{:S(2)}) copy-start(f32[5120]{0:T(1024)} %param.7) | copy-start | bytes 61444
  22.9 6.1 %copy-start.2 = (f32[5120]{0:T(1024)S(1)}, f32[5120]{0:T(1024)}, u32[]{:S(2)}) copy-start(f32[5120]{0:T(1024)} %param.9) | copy-start | bytes 61444
  22.9 6.0 %collective-permute-start.4 = (bf16[5120]{0:T(1024)(128)(2,1)S(1)}, bf16[5120]{0:T(1024)(128)(2,1)S(1)}, u32[]{:S(2)}, u32[]{:S(2)}) collective-permute-start(bf16[5120]{0:T(1024)(128)(2,1)S(1)} %select_convert_fusion.3), channel_id=1, source_target_pairs={{0,1},{1,0},{2,3},{3,2},{4,5},{5,4},{6,7},{7,6},{8,9},{9,8},{10,11... | collective-permute-start | bytes 30728 | tf_op jit(solution)/shard_map/ppermute | solution.py:12
  28.1 0.7 copy-start.4
where the time goes:
time: 116 us; the launch traced here: 115 us
  blocking collectives  81.1 us (70%)
  waiting for transfers between devices  12.9 us (11%)
  starting transfers between devices  11.1 us (10%)
  other arithmetic  6.59 us (6%)
  between operations  2.19 us (2%)
  local copies, waits for them, and re-layouts  1.42 us (1%)
    all_gather x1, blocking collectives, body(): lax.all_gather(new_master.astype(jnp.bfloat16), 'dp', axis=0, tiled=True)  42.4 us
    psum x1, blocking collectives, body(): wsq, usq = lax.psum((local_wsq, local_usq), 'dp')  38.7 us
    ppermute x5, waiting for transfers between devices, swapped(): return lax.ppermute(value, axis, pairs)  12.9 us
    ppermute x5, starting transfers between devices, swapped(): return lax.ppermute(value, axis, pairs)  11.1 us
  transfers between devices with their start and end apart: 5, of which 4 were waited for; matrix products, arithmetic and copies ran while one was open for 0% of the time, Pallas kernels for 0%

commit v1 on v0

v1 whole, which is shorter than its diff:
```python
import functools

import jax
import jax.numpy as jnp
import numpy as np
from jax import lax
from jax.experimental import pallas as pl
from jax.experimental.pallas import tpu as pltpu
from jax.sharding import PartitionSpec as P

LANES = 128
BETA1, BETA2 = 0.9, 0.999
STEP_BITS = 8


def levels(count):
    chips = count // 2
    bits = chips.bit_length() - 1
    plane = 1 << ((bits + 1) // 2)
    return chips // plane, plane


def flipped(value, mask):
    bit = 1
    while bit <= mask:
        if mask & bit:
            value = value + bit * (1 - 2 * (value // bit % 2))
        bit *= 2
    return value


def power(base, step):
    result = jnp.ones(step.shape, jnp.float32)
    for bit in range(STEP_BITS):
        factor = float(np.float32(float(np.float32(base)) ** (2**bit)))
        result = result * jnp.where((step // 2**bit) % 2 == 1, factor, 1.0)
    return result


def kernel(
    count, line, plane, width,
    grads, master, moment1, moment2, rows_ref, step_ref,
    weights_out, master_out, moment1_out, moment2_out,
    theirs, ours, pair_send, pair_recv, own, plane_send, plane_recv,
    total, line_send, line_recv, masters, updates, m1, m2, m1_new, m2_new,
    master_new, weights, wsums, usums, ratios,
    local_sem, send_sem, recv_sem,
):
    me = lax.axis_index("dp")
    core = me % 2
    xy = me // 2 % plane
    z = me // (2 * plane)
    other = 1 - core
    order = list(range(plane - 1, -1, -1))
    far_first = list(range(line - 1, 0, -1))
    partner = me + 1 - 2 * core

    def plane_peer(mask):
        return (z * plane + flipped(xy, mask)) * 2 + core

    def line_peer(mask):
        return (flipped(z, mask) * plane + xy) * 2 + core

    peers = [partner] + [plane_peer(k) for k in range(1, plane)]
    peers += [line_peer(k) for k in range(1, line)]
    barrier = pltpu.get_barrier_semaphore()
    for peer in peers:
        pl.semaphore_signal(barrier, inc=1, device_id=(peer,), device_id_type=pl.DeviceIdType.MESH)

    used = {"local": 0, "remote": 0}
    sent = []

    def local(source, target):
        copy = pltpu.make_async_copy(source, target, local_sem.at[used["local"]])
        used["local"] += 1
        copy.start()
        return copy

    def remote(source, target, peer):
        slot = used["remote"]
        used["remote"] += 1
        copy = pltpu.make_async_remote_copy(
            src_ref=source, dst_ref=target,
            send_sem=send_sem.at[slot], recv_sem=recv_sem.at[slot],
            device_id=(peer,), device_id_type=pl.DeviceIdType.MESH,
        )
        copy.start()
        sent.append(copy)
        return copy

    their_loads = [local(grads.at[:, flipped(xy, k), other], theirs.at[k]) for k in order]
    master_load = local(master, masters.at[core, xy, z])
    our_loads = [local(grads.at[:, flipped(xy, k), core], ours.at[k]) for k in order]
    m1_load = local(moment1, m1)
    m2_load = local(moment2, m2)

    for k, load in zip(order, their_loads):
        load.wait()
        pair_send[k] = theirs[k].reshape(line * width, LANES).astype(jnp.bfloat16)
    master_load.wait()
    pl.semaphore_wait(barrier, len(peers))

    pair_copies = [remote(pair_send.at[k], pair_recv.at[k], partner) for k in order]
    row = masters.at[core, xy, z]
    master_line = [remote(row, row, line_peer(k)) for k in far_first]

    plane_copies = []
    for k, load, copy in zip(order, our_loads, pair_copies):
        load.wait()
        copy.wait_recv()
        chip = ours[k].reshape(line * width, LANES) + pair_recv[k].astype(jnp.float32)
        if k:
            plane_send[k - 1] = chip.astype(jnp.bfloat16)
            plane_copies.append((k, remote(plane_send.at[k - 1], plane_recv.at[k - 1], plane_peer(k))))
        else:
            own[...] = chip

    for copy in master_line:
        copy.wait_recv()
    column = masters.at[core, xy]
    master_plane = [(k, remote(column, column, plane_peer(k))) for k in order if k]
    master_pair = [remote(column, column, partner)]

    acc = own[...]
    for k, copy in plane_copies:
        copy.wait_recv()
        acc = acc + plane_recv[k - 1].astype(jnp.float32)
    total[...] = acc.reshape(line, width, LANES)
    line_copies = []
    for k in far_first:
        line_send[k - 1] = total[flipped(z, k)].astype(jnp.bfloat16)
        line_copies.append((k, remote(line_send.at[k - 1], line_recv.at[k - 1], line_peer(k))))

    m1_load.wait()
    m2_load.wait()
    step = jnp.full((8, LANES), step_ref[0], jnp.int32)
    first_scale = (1.0 - power(BETA1, step))[:1]
    second_scale = (1.0 - power(BETA2, step))[:1]
    grad = total[z]
    for k, copy in line_copies:
        copy.wait_recv()
        grad = grad + line_recv[k - 1].astype(jnp.float32)
    grad = grad / jnp.float32(count)
    new_m1 = 0.9 * m1[...] + 0.1 * grad
    new_m2 = 0.999 * m2[...] + 0.001 * grad * grad
    update = (new_m1 / first_scale) / (jnp.sqrt(new_m2 / second_scale) + 1e-06)
    updates[core, xy, z] = update + 0.1 * masters[core, xy, z]
    row = updates.at[core, xy, z]
    update_line = [remote(row, row, line_peer(k)) for k in far_first]
    m1_new[...] = new_m1
    m2_new[...] = new_m2
    stores = [local(m1_new, moment1_out), local(m2_new, moment2_out)]

    def square_sums(table, sums, side, at):
        start = (side * plane + at) * line
        for j in range(line):
            values = table[side, at, j].reshape(width // 8, 8, LANES)
            sums[start + j] = jnp.sum(values * values, axis=0)

    square_sums(masters, wsums, core, xy)
    for k, copy in master_plane:
        copy.wait_recv()
        at = flipped(xy, k)
        chunk = masters.at[core, at]
        master_pair.append(remote(chunk, chunk, partner))
        square_sums(masters, wsums, core, at)

    for copy in update_line:
        copy.wait_recv()
    column = updates.at[core, xy]
    update_plane = [(k, remote(column, column, plane_peer(k))) for k in order if k]
    update_pair = [remote(column, column, partner)]
    square_sums(updates, usums, core, xy)

    pair_masks = [0] + [k for k in order if k]
    for k, copy in zip(pair_masks, master_pair):
        copy.wait_recv()
        square_sums(masters, wsums, other, flipped(xy, k))

    index0 = lax.broadcasted_iota(jnp.int32, (count, count), 0)
    index1 = lax.broadcasted_iota(jnp.int32, (count, count), 1)

    def tensor_of(index):
        natural = (index % line * plane + index // line % plane) * 2 + index // (line * plane)
        end = jnp.int32(0)
        tensor = jnp.zeros(index.shape, jnp.int32)
        for k in range(rows_ref.shape[0]):
            end = end + rows_ref[k]
            tensor = tensor + (natural >= end).astype(jnp.int32)
        return tensor

    same = tensor_of(index0) == tensor_of(index1)

    def over_tensor(sums):
        per_row = jnp.sum(jnp.sum(sums[...], axis=1), axis=1, keepdims=True)
        return jnp.sum(jnp.where(same, per_row, 0.0), axis=0, keepdims=True)

    wsq = over_tensor(wsums)

    for k, copy in update_plane:
        copy.wait_recv()
        at = flipped(xy, k)
        chunk = updates.at[core, at]
        update_pair.append(remote(chunk, chunk, partner))
        square_sums(updates, usums, core, at)
    for k, copy in zip(pair_masks, update_pair):
        copy.wait_recv()
        square_sums(updates, usums, other, flipped(xy, k))

    ratio = jnp.sqrt(wsq / (over_tensor(usums) + 1e-06))
    column = jnp.sum(jnp.where(index0 == index1, ratio, 0.0), axis=1, keepdims=True)
    ratios[...] = jnp.broadcast_to(0.2 * column, (count, LANES))

    def new_row(side, at, j):
        scale = ratios[pl.ds((side * plane + at) * line + j, 1), :]
        return masters[side, at, j] - scale * updates[side, at, j]

    master_new[...] = new_row(core, xy, z)
    stores.append(local(master_new, master_out))

    base = used["local"]

    @pl.loop(0, line)
    def _(j):
        for at in range(plane):
            both = jnp.concatenate([new_row(0, at, j), new_row(1, at, j)], axis=0)
            weights[j, at] = both.astype(jnp.bfloat16)
        pltpu.make_async_copy(weights.at[j], weights_out.at[j], local_sem.at[base + j]).start()

    for j in range(line):
        stores.append(pltpu.make_async_copy(weights.at[j], weights_out.at[j], local_sem.at[base + j]))
    for copy in stores:
        copy.wait()
    for copy in sent:
        copy.wait_send()


def body(grads, master, moment1, moment2, tensor_rows, step_count):
    count = lax.axis_size("dp")
    line, plane = levels(count)
    width = master.shape[0] // LANES
    row = (width, LANES)
    f32, bf16 = jnp.float32, jnp.bfloat16
    anywhere = pl.BlockSpec(memory_space=pl.ANY)
    scalars = pl.BlockSpec(memory_space=pltpu.SMEM)
    tall = (line * width, LANES)
    remotes = plane + 3 * (line - 1 + plane - 1) + 2 * plane
    outs = pl.pallas_call(
        functools.partial(kernel, count, line, plane, width),
        out_shape=(
            jax.ShapeDtypeStruct((line, plane, 2 * width, LANES), bf16),
            jax.ShapeDtypeStruct(row, f32),
            jax.ShapeDtypeStruct(row, f32),
            jax.ShapeDtypeStruct(row, f32),
        ),
        in_specs=[anywhere] * 4 + [scalars] * 2,
        out_specs=(anywhere,) * 4,
        scratch_shapes=[
            pltpu.VMEM((plane, line) + row, f32),
            pltpu.VMEM((plane, line) + row, f32),
            pltpu.VMEM((plane,) + tall, bf16),
            pltpu.VMEM((plane,) + tall, bf16),
            pltpu.VMEM(tall, f32),
            pltpu.VMEM((plane - 1,) + tall, bf16),
            pltpu.VMEM((plane - 1,) + tall, bf16),
            pltpu.VMEM((line,) + row, f32),
            pltpu.VMEM((line - 1,) + row, bf16),
            pltpu.VMEM((line - 1,) + row, bf16),
            pltpu.VMEM((2, plane, line) + row, f32),
            pltpu.VMEM((2, plane, line) + row, f32),
            pltpu.VMEM(row, f32),
            pltpu.VMEM(row, f32),
            pltpu.VMEM(row, f32),
            pltpu.VMEM(row, f32),
            pltpu.VMEM(row, f32),
            pltpu.VMEM((line, plane, 2 * width, LANES), bf16),
            pltpu.VMEM((count, 8, LANES), f32),
            pltpu.VMEM((count, 8, LANES), f32),
            pltpu.VMEM((count, LANES), f32),
            pltpu.SemaphoreType.DMA((2 * plane + 6 + line,)),
            pltpu.SemaphoreType.DMA((remotes,)),
            pltpu.SemaphoreType.DMA((remotes,)),
        ],
        compiler_params=pltpu.CompilerParams(
            collective_id=0, has_side_effects=True, vmem_limit_bytes=48 * 1024 * 1024
        ),
        name="lamb",
    )(
        grads.reshape(line, plane, 2, width, LANES),
        master.reshape(row), moment1.reshape(row), moment2.reshape(row),
        tensor_rows, step_count,
    )
    return tuple(out.reshape(-1) for out in outs)


def solution(mesh):
    placed = (P("dp", None), P("dp"), P("dp"), P("dp"), P(), P())
    return jax.shard_map(
        body,
        mesh=mesh,
        in_specs=placed,
        out_specs=(P(), P("dp"), P("dp"), P("dp")),
        check_vma=False,
    )
```

time: 116 us -> 33.2 us (0.29)
  blocking collectives: 81.1 us -> 0 us
  Pallas kernels: 0 us -> 25.1 us
  waiting for transfers between devices: 12.9 us -> 0 us
  starting transfers between devices: 11.1 us -> 0 us
  other arithmetic: 6.59 us -> 0 us
  local copies, waits for them, and re-layouts: 1.42 us -> 6.49 us
    all_gather x1 -> x0, blocking collectives: 42.4 us -> none  [body(): lax.all_gather(new_master.astype(jnp.bfloat16), 'dp', axis=0, tiled=True)]
    psum x1 -> x0, blocking collectives: 38.7 us -> none  [body(): wsq, usq = lax.psum((local_wsq, local_usq), 'dp')]
    pallas_call x0 -> x1, Pallas kernels: none -> 25.1 us  [body(): pl.pallas_call(functools.partial(kernel, count, line, plane, width), out_...]
    ppermute x5 -> x0, waiting for transfers between devices: 12.9 us -> none  [swapped(): return lax.ppermute(value, axis, pairs)]
    ppermute x5 -> x0, starting transfers between devices: 11.1 us -> none  [swapped(): return lax.ppermute(value, axis, pairs)]
    unnamed x11 -> x14, local copies, waits for them, and re-layouts: 1.42 us -> 6.49 us
    convert_element_type x6 -> x0, other arithmetic: 2.81 us -> none  [the longest x5 2.2 us: body(): give.astype(jnp.bfloat16)]
    reduce_sum x2 -> x0, other arithmetic: 1.93 us -> none  [the longest x1 1.31 us: tensor_sums(): row_sums = jnp.sum(rows * rows, axis=1)]
  transfers between devices with their start and end apart: 5 -> 0, of which waited for: 4 -> 0; matrix products, arithmetic and copies ran while one was open for 0% -> 0% of each run, Pallas kernels for 0% -> 0%
where the time goes in v1:
time: 33.2 us; the launch traced here: 32.9 us
  Pallas kernels  25.1 us (76%)
  local copies, waits for them, and re-layouts  6.49 us (20%)
  between operations  1.3 us (4%)
    pallas_call x1, Pallas kernels, body(): pl.pallas_call(functools.partial(kernel, count, line, plane, width), out_...  25.1 us
    unnamed x14, local copies, waits for them, and re-layouts  6.49 us

profile of v1, /device:TPU:1, one launch (start us, length us, event | category | flops | bytes accessed | tf_op | source)
XLA Modules:
  0.0 32.9 jit_solution(621495120111938623)
XLA Ops:
  1.3 0.0 copy-start.4
  1.3 0.6 %copy-done.4 = s32[8]{0:T(128)S(1)} copy-done((s32[8]{0:T(128)S(1)}, s32[8]{0:T(128)}, u32[]{:S(2)}) %copy-start.4) | copy-done | bytes 56
  1.9 0.0 copy-start
  1.9 1.1 %copy-done = f32[1,163840]{1,0:T(1,128)S(1)} copy-done((f32[1,163840]{1,0:T(1,128)S(1)}, f32[1,163840]{1,0:T(1,128)}, u32[]{:S(2)}) %copy-start) | copy-done | bytes 655384
  3.0 0.0 copy-start.1
  3.0 0.7 %copy-done.1 = f32[5120]{0:T(1024)S(1)} copy-done((f32[5120]{0:T(1024)S(1)}, f32[5120]{0:T(1024)}, u32[]{:S(2)}) %copy-start.1) | copy-done | bytes 20504
  3.8 0.0 copy-start.2
  3.8 0.7 %copy-done.2 = f32[5120]{0:T(1024)S(1)} copy-done((f32[5120]{0:T(1024)S(1)}, f32[5120]{0:T(1024)}, u32[]{:S(2)}) %copy-start.2) | copy-done | bytes 20504
  4.5 0.0 copy-start.3
  4.5 0.7 %copy-done.3 = f32[5120]{0:T(1024)S(1)} copy-done((f32[5120]{0:T(1024)S(1)}, f32[5120]{0:T(1024)}, u32[]{:S(2)}) %copy-start.3) | copy-done | bytes 20504
  5.2 25.1 %lamb.1 = (bf16[4,4,80,128]{3,2,1,0:T(8,128)(2,1)S(1)}, f32[40,128]{1,0:T(8,128)S(1)}, f32[40,128]{1,0:T(8,128)S(1)}, f32[40,128]{1,0:T(8,128)S(1)}) custom-call(f32[4,4,2,40,128]{4,3,2,1,0:T(8,128)S(1)} %bitcast.8, f32[40,128]{1,0:T(8,128)S(1)} %bitcast.10, f32[40,128]{1,0:T(8,128)S(1)} %bitcast.11, f32[40,128]{1,0:T(8,128)S(1)} %bitcast.12, ...), custom_call_target="tpu_custom_call" | custom-call | tf_op jit(solution)/shard_map/lamb/pallas_call | solution.py:248
  30.3 0.7 %copy.15 = bf16[163840]{0:T(1024)(128)(2,1)} copy(bf16[163840]{0:T(1024)(128)(2,1)S(1)} %bitcast.9) | data formatting | bytes 655360
  31.1 0.6 %copy.16 = f32[5120]{0:T(1024)} copy(f32[5120]{0:T(1024)S(1)} %bitcast.15) | data formatting | bytes 40960
  31.7 0.6 %copy.17 = f32[5120]{0:T(1024)} copy(f32[5120]{0:T(1024)S(1)} %bitcast.14) | data formatting | bytes 40960
  32.3 0.6 %copy.18 = f32[5120]{0:T(1024)} copy(f32[5120]{0:T(1024)S(1)} %bitcast.13) | data formatting | bytes 40960
Async XLA Ops:
  1.3 0.7 %copy-start.4 = (s32[8]{0:T(128)S(1)}, s32[8]{0:T(128)}, u32[]{:S(2)}) copy-start(s32[8]{0:T(128)} %rows_ref.1) | copy-start | bytes 100
  1.9 1.1 %copy-start = (f32[1,163840]{1,0:T(1,128)S(1)}, f32[1,163840]{1,0:T(1,128)}, u32[]{:S(2)}) copy-start(f32[1,163840]{1,0:T(1,128)} %param.6) | copy-start | bytes 1966084
  3.0 0.7 %copy-start.1 = (f32[5120]{0:T(1024)S(1)}, f32[5120]{0:T(1024)}, u32[]{:S(2)}) copy-start(f32[5120]{0:T(1024)} %param.7) | copy-start | bytes 61444
  3.8 0.7 %copy-start.2 = (f32[5120]{0:T(1024)S(1)}, f32[5120]{0:T(1024)}, u32[]{:S(2)}) copy-start(f32[5120]{0:T(1024)} %param.8) | copy-start | bytes 61444
  4.5 0.7 %copy-start.3 = (f32[5120]{0:T(1024)S(1)}, f32[5120]{0:T(1024)}, u32[]{:S(2)}) copy-start(f32[5120]{0:T(1024)} %param.9) | copy-start | bytes 61444

commit v2 on v1

v2 whole, which is shorter than its diff:
```python
import functools

import jax
import jax.numpy as jnp
import numpy as np
from jax import lax
from jax.experimental import pallas as pl
from jax.experimental.pallas import tpu as pltpu
from jax.sharding import PartitionSpec as P

LANES = 128
BETA1, BETA2 = 0.9, 0.999
STEP_BITS = 8


def levels(count):
    chips = count // 2
    bits = chips.bit_length() - 1
    plane = 1 << ((bits + 1) // 2)
    return chips // plane, plane


def flipped(value, mask):
    bit = 1
    while bit <= mask:
        if mask & bit:
            value = value + bit * (1 - 2 * (value // bit % 2))
        bit *= 2
    return value


def power(base, step):
    result = jnp.ones(step.shape, jnp.float32)
    for bit in range(STEP_BITS):
        factor = float(np.float32(float(np.float32(base)) ** (2**bit)))
        result = result * jnp.where((step // 2**bit) % 2 == 1, factor, 1.0)
    return result


def kernel(
    count, line, plane,
    grads, master, moment1, moment2, rows_in, step_ref,
    masters, updates, ratios, m1_new, m2_new,
    theirs, ours, pair_send, pair_recv, plane_send, plane_recv,
    line_send, line_recv, m1, m2, wsums, usums, rows_ref,
    local_sem, send_sem, recv_sem,
):
    me = lax.axis_index("dp")
    core = me % 2
    xy = me // 2 % plane
    z = me // (2 * plane)
    other = 1 - core
    partner = me + 1 - 2 * core
    far_first = list(range(line - 1, 0, -1))
    diagonal_first = list(range(plane - 1, 0, -1))

    def plane_peer(mask):
        return (z * plane + flipped(xy, mask)) * 2 + core

    def line_peer(mask):
        return (flipped(z, mask) * plane + xy) * 2 + core

    peers = [partner] + [plane_peer(k) for k in range(1, plane)]
    peers += [line_peer(k) for k in range(1, line)]
    barrier = pltpu.get_barrier_semaphore()
    for peer in peers:
        pl.semaphore_signal(barrier, inc=1, device_id=(peer,), device_id_type=pl.DeviceIdType.MESH)

    used = {"local": 0, "remote": 0}
    sent = []

    def local(source, target):
        copy = pltpu.make_async_copy(source, target, local_sem.at[used["local"]])
        used["local"] += 1
        copy.start()
        return copy

    def remote(source, target, peer):
        slot = used["remote"]
        used["remote"] += 1
        copy = pltpu.make_async_remote_copy(
            src_ref=source, dst_ref=target,
            send_sem=send_sem.at[slot], recv_sem=recv_sem.at[slot],
            device_id=(peer,), device_id_type=pl.DeviceIdType.MESH,
        )
        copy.start()
        sent.append(copy)
        return copy

    def share(ref, peer):
        return remote(ref, ref, peer)

    layers = far_first + [0]
    their_loads = [local(grads.at[flipped(z, k), :, other], theirs.at[k]) for k in layers]
    master_load = local(master, masters.at[core, xy, z])
    our_loads = [local(grads.at[flipped(z, k), :, core], ours.at[k]) for k in layers]
    small_loads = [
        local(moment1, m1), local(moment2, m2), local(rows_in, rows_ref)
    ]

    for k, load in zip(layers, their_loads):
        load.wait()
        pair_send[k] = theirs[k].astype(jnp.bfloat16)
    master_load.wait()
    pl.semaphore_wait(barrier, len(peers))

    pair_copies = [remote(pair_send.at[k], pair_recv.at[k], partner) for k in layers]
    master_line = [share(masters.at[core, xy, z], line_peer(k)) for k in far_first]

    plane_copies = {}
    for k, load, copy in zip(layers, our_loads, pair_copies):
        load.wait()
        copy.wait_recv()
        for p in diagonal_first:
            at = flipped(xy, p)
            chip = ours[k, at] + pair_recv[k, at].astype(jnp.float32)
            plane_send[k, p - 1] = chip.astype(jnp.bfloat16)
            plane_copies[k, p] = remote(plane_send.at[k, p - 1], plane_recv.at[k, p - 1], plane_peer(p))

    def plane_sum(k):
        total = ours[k, xy] + pair_recv[k, xy].astype(jnp.float32)
        for p in diagonal_first:
            plane_copies[k, p].wait_recv()
            total = total + plane_recv[k, p - 1].astype(jnp.float32)
        return total

    line_copies = []
    for k in far_first:
        line_send[k - 1] = plane_sum(k).astype(jnp.bfloat16)
        line_copies.append((k, remote(line_send.at[k - 1], line_recv.at[k - 1], line_peer(k))))

    grad = plane_sum(0)
    for copy in small_loads:
        copy.wait()
    step = jnp.full((8, LANES), step_ref[0], jnp.int32)
    first_scale = 1.0 - power(BETA1, step)
    second_scale = 1.0 - power(BETA2, step)

    for copy in master_line:
        copy.wait_recv()
    column = masters.at[core, xy]
    master_plane = [(p, share(column, plane_peer(p))) for p in diagonal_first]
    master_pair = [share(column, partner)]

    for k, copy in line_copies:
        copy.wait_recv()
        grad = grad + line_recv[k - 1].astype(jnp.float32)
    grad = grad / jnp.float32(count)
    new_m1 = 0.9 * m1[...] + 0.1 * grad
    new_m2 = 0.999 * m2[...] + 0.001 * grad * grad
    update = (new_m1 / first_scale) / (jnp.sqrt(new_m2 / second_scale) + 1e-06)
    updates[core, xy, z] = update + 0.1 * masters[core, xy, z]
    m1_new[...] = new_m1
    m2_new[...] = new_m2

    update_line = [(k, share(updates.at[core, xy, z], line_peer(k))) for k in far_first]
    update_plane, update_pair = [], []

    def spread(at_z):
        row = updates.at[core, xy, at_z]
        for p in diagonal_first:
            update_plane.append((p, at_z, share(row, plane_peer(p))))
        update_pair.append((xy, at_z, share(row, partner)))

    def square_sum(table, sums, side, at, j):
        values = table[side, at, j]
        sums[(side * plane + at) * line + j] = jnp.sum(values * values, axis=0)

    def square_sums(table, sums, side, at):
        for j in range(line):
            square_sum(table, sums, side, at, j)

    spread(z)
    square_sums(masters, wsums, core, xy)
    for p, copy in master_plane:
        copy.wait_recv()
        at = flipped(xy, p)
        master_pair.append(share(masters.at[core, at], partner))
        square_sums(masters, wsums, core, at)
    for k, copy in reversed(update_line):
        copy.wait_recv()
        spread(flipped(z, k))
    square_sums(updates, usums, core, xy)
    for p, at_z, copy in update_plane:
        copy.wait_recv()
        at = flipped(xy, p)
        update_pair.append((at, at_z, share(updates.at[core, at, at_z], partner)))
        square_sum(updates, usums, core, at, at_z)

    for p, copy in zip([0] + diagonal_first, master_pair):
        copy.wait_recv()
        square_sums(masters, wsums, other, flipped(xy, p))

    index0 = lax.broadcasted_iota(jnp.int32, (count, count), 0)
    index1 = lax.broadcasted_iota(jnp.int32, (count, count), 1)

    def tensor_of(index):
        natural = (index % line * plane + index // line % plane) * 2 + index // (line * plane)
        end = jnp.int32(0)
        tensor = jnp.zeros(index.shape, jnp.int32)
        for k in range(rows_ref.shape[0]):
            end = end + rows_ref[k]
            tensor = tensor + (natural >= end).astype(jnp.int32)
        return tensor

    same = tensor_of(index0) == tensor_of(index1)

    def over_tensor(sums):
        per_row = jnp.sum(jnp.sum(sums[...], axis=1), axis=1, keepdims=True)
        return jnp.sum(jnp.where(same, per_row, 0.0), axis=0, keepdims=True)

    wsq = over_tensor(wsums)

    for at, at_z, copy in update_pair:
        copy.wait_recv()
        square_sum(updates, usums, other, at, at_z)

    ratio = jnp.sqrt(wsq / (over_tensor(usums) + 1e-06))
    column = jnp.sum(jnp.where(index0 == index1, ratio, 0.0), axis=1, keepdims=True)
    ratios[...] = jnp.broadcast_to(0.2 * column, (count, LANES))
    for copy in sent:
        copy.wait_send()


def finish(
    line, plane,
    masters, updates, ratios, m1_new, m2_new,
    weights_out, master_out, moment1_out, moment2_out,
    weights, master_new, sem,
):
    me = lax.axis_index("dp")
    copies = [
        pltpu.make_async_copy(m1_new, moment1_out, sem.at[0]),
        pltpu.make_async_copy(m2_new, moment2_out, sem.at[1]),
    ]
    for copy in copies:
        copy.start()

    def new_row(side, at, j):
        scale = ratios[pl.ds((side * plane + at) * line + j, 1), :]
        return masters[side, at, j] - scale * updates[side, at, j]

    master_new[...] = new_row(me % 2, me // 2 % plane, me // (2 * plane))
    copies.append(pltpu.make_async_copy(master_new, master_out, sem.at[2]))
    copies[-1].start()

    @pl.loop(0, line)
    def _(j):
        for at in range(plane):
            for side in range(2):
                weights[j, at, side] = new_row(side, at, j).astype(jnp.bfloat16)
        pltpu.make_async_copy(weights.at[j], weights_out.at[j], sem.at[3 + j]).start()

    for j in range(line):
        copies.append(pltpu.make_async_copy(weights.at[j], weights_out.at[j], sem.at[3 + j]))
    for copy in copies:
        copy.wait()


def pinned(array):
    return pltpu.with_memory_space_constraint(array, pltpu.HBM)


def body(grads, master, moment1, moment2, tensor_rows, step_count):
    count = lax.axis_size("dp")
    line, plane = levels(count)
    row = (master.shape[0] // (8 * LANES), 8, LANES)
    f32, bf16 = jnp.float32, jnp.bfloat16
    hbm = pl.BlockSpec(memory_space=pltpu.HBM)
    vmem = pl.BlockSpec(memory_space=pltpu.VMEM)
    table = (2, plane, line) + row
    remotes = line + line * (plane - 1) + 2 * (line - 1) + plane - 1 + plane
    remotes += line - 1 + line * (plane - 1) + line * plane
    state = pl.pallas_call(
        functools.partial(kernel, count, line, plane),
        out_shape=(
            jax.ShapeDtypeStruct(table, f32),
            jax.ShapeDtypeStruct(table, f32),
            jax.ShapeDtypeStruct((count, LANES), f32),
            jax.ShapeDtypeStruct(row, f32),
            jax.ShapeDtypeStruct(row, f32),
        ),
        in_specs=[hbm] * 5 + [pl.BlockSpec(memory_space=pltpu.SMEM)],
        out_specs=(vmem,) * 5,
        scratch_shapes=[
            pltpu.VMEM((line, plane) + row, f32),
            pltpu.VMEM((line, plane) + row, f32),
            pltpu.VMEM((line, plane) + row, bf16),
            pltpu.VMEM((line, plane) + row, bf16),
            pltpu.VMEM((line, plane - 1) + row, bf16),
            pltpu.VMEM((line, plane - 1) + row, bf16),
            pltpu.VMEM((line - 1,) + row, bf16),
            pltpu.VMEM((line - 1,) + row, bf16),
            pltpu.VMEM(row, f32),
            pltpu.VMEM(row, f32),
            pltpu.VMEM((count, 8, LANES), f32),
            pltpu.VMEM((count, 8, LANES), f32),
            pltpu.SMEM(tensor_rows.shape, jnp.int32),
            pltpu.SemaphoreType.DMA((2 * line + 4,)),
            pltpu.SemaphoreType.DMA((remotes,)),
            pltpu.SemaphoreType.DMA((remotes,)),
        ],
        compiler_params=pltpu.CompilerParams(
            collective_id=0, has_side_effects=True, vmem_limit_bytes=40 * 1024 * 1024
        ),
        name="exchange",
    )(
        pinned(grads.reshape((line, plane, 2) + row)),
        pinned(master.reshape(row)), pinned(moment1.reshape(row)), pinned(moment2.reshape(row)),
        pinned(tensor_rows), step_count,
    )
    outs = pl.pallas_call(
        functools.partial(finish, line, plane),
        out_shape=(
            jax.ShapeDtypeStruct((line, plane, 2) + row, bf16),
            jax.ShapeDtypeStruct(row, f32),
            jax.ShapeDtypeStruct(row, f32),
            jax.ShapeDtypeStruct(row, f32),
        ),
        in_specs=[vmem] * 5,
        out_specs=(hbm,) * 4,
        scratch_shapes=[
            pltpu.VMEM((line, plane, 2) + row, bf16),
            pltpu.VMEM(row, f32),
            pltpu.SemaphoreType.DMA((3 + line,)),
        ],
        compiler_params=pltpu.CompilerParams(vmem_limit_bytes=24 * 1024 * 1024),
        name="finish",
    )(*state)
    return tuple(out.reshape(-1) for out in outs)


def solution(mesh):
    placed = (P("dp", None), P("dp"), P("dp"), P("dp"), P(), P())
    return jax.shard_map(
        body,
        mesh=mesh,
        in_specs=placed,
        out_specs=(P(), P("dp"), P("dp"), P("dp")),
        check_vma=False,
    )
```

time: 33.2 us -> 25.2 us (0.76)
  local copies, waits for them, and re-layouts: 6.49 us -> 0 us
  Pallas kernels: 25.1 us -> 23.7 us
    unnamed x14 -> x0, local copies, waits for them, and re-layouts: 6.49 us -> none
    pallas_call x1 -> x2, Pallas kernels: 25.1 us -> 23.7 us  [the longest x1 22.9 us: body(): pl.pallas_call(functools.partial(kernel, count, line, plane), out_shape=(...]
where the time goes in v2:
time: 25.2 us; the launch traced here: 25 us
  Pallas kernels  23.7 us (94%)
  between operations  1.29 us (5%)
    pallas_call x1, Pallas kernels, body(): pl.pallas_call(functools.partial(kernel, count, line, plane), out_shape=(...  22.9 us
    pallas_call x1, Pallas kernels, body(): pl.pallas_call(functools.partial(finish, line, plane), out_shape=(jax.Sha...  0.83 us

profile of v2, /device:TPU:1, one launch (start us, length us, event | category | flops | bytes accessed | tf_op | source)
XLA Modules:
  0.0 25.0 jit_solution(5309262275019724674)
XLA Ops:
  1.3 22.9 %exchange.1 = (f32[2,4,4,5,8,128]{5,4,3,2,1,0:T(8,128)S(1)}, f32[2,4,4,5,8,128]{5,4,3,2,1,0:T(8,128)S(1)}, f32[32,128]{1,0:T(8,128)S(1)}, f32[5,8,128]{2,1,0:T(8,128)S(1)}, f32[5,8,128]{2,1,0:T(8,128)S(1)}) custom-call(f32[4,4,2,5,8,128]{5,4,3,2,1,0:T(8,128)} %bitcast.8, f32[5,8,128]{2,1,0:T(8,128)} %bitcast.9, f32[5,8,128]{2,1,0:T(8,128)} %bitcast.10, ...), custom_call_target="tpu_custom_call" | custom-call | tf_op jit(solution)/shard_map/exchange/pallas_call | solution.py:274
  24.2 0.8 %finish.1 = (bf16[4,4,2,5,8,128]{5,4,3,2,1,0:T(8,128)(2,1)}, f32[5,8,128]{2,1,0:T(8,128)}, f32[5,8,128]{2,1,0:T(8,128)}, f32[5,8,128]{2,1,0:T(8,128)}) custom-call(f32[2,4,4,5,8,128]{5,4,3,2,1,0:T(8,128)S(1)} %get-tuple-element.13.masters, f32[2,4,4,5,8,128]{5,4,3,2,1,0:T(8,128)S(1)} %get-tuple-element.14.updates, f32[32,128]{1,0:T(8,128)S(1)} %get-tuple-element.15.ratios, ...), custom_call_target="tpu_custom_call" | custom-call | tf_op jit(solution)/shard_map/finish/pallas_call | solution.py:312

commit v3 on v2

--- a/solution.py
+++ b/solution.py
@@ -40,7 +40,7 @@
 def kernel(
     count, line, plane,
     grads, master, moment1, moment2, rows_in, step_ref,
-    masters, updates, ratios, m1_new, m2_new,
+    masters, guesses, deltas, ratios, m1_new, m2_new, mine,
     theirs, ours, pair_send, pair_recv, plane_send, plane_recv,
     line_send, line_recv, m1, m2, wsums, usums, rows_ref,
     local_sem, send_sem, recv_sem,
@@ -94,9 +94,15 @@
     their_loads = [local(grads.at[flipped(z, k), :, other], theirs.at[k]) for k in layers]
     master_load = local(master, masters.at[core, xy, z])
     our_loads = [local(grads.at[flipped(z, k), :, core], ours.at[k]) for k in layers]
-    small_loads = [
-        local(moment1, m1), local(moment2, m2), local(rows_in, rows_ref)
-    ]
+    moment_loads = [local(moment1, m1), local(moment2, m2)]
+    rows_load = local(rows_in, rows_ref)
+    step = jnp.full((8, LANES), step_ref[0], jnp.int32)
+    first_scale = 1.0 - power(BETA1, step)
+    second_scale = 1.0 - power(BETA2, step)
+
+    def update_of(first, second, weight):
+        return (first / first_scale) / (jnp.sqrt(second / second_scale) + 1e-06) + 0.1 * weight
+
 
     for k, load in zip(layers, their_loads):
         load.wait()
@@ -105,7 +111,22 @@
     pl.semaphore_wait(barrier, len(peers))
 
     pair_copies = [remote(pair_send.at[k], pair_recv.at[k], partner) for k in layers]
-    master_line = [share(masters.at[core, xy, z], line_peer(k)) for k in far_first]
+    early = (masters, guesses)
+    early_line = {k: [share(masters.at[core, xy, z], line_peer(k))] for k in far_first}
+    for copy in moment_loads:
+        copy.wait()
+    guess = update_of(0.9 * m1[...], 0.999 * m2[...], masters[core, xy, z]).astype(jnp.bfloat16)
+    guesses[core, xy, z] = guess
+    early_plane = {p: [] for p in diagonal_first}
+
+    def early_spread(at_z):
+        for p in diagonal_first:
+            for table in early:
+                early_plane[p].append(share(table.at[core, xy, at_z], plane_peer(p)))
+
+    for k in far_first:
+        early_line[k].append(share(guesses.at[core, xy, z], line_peer(k)))
+    early_spread(z)
 
     plane_copies = {}
     for k, load, copy in zip(layers, our_loads, pair_copies):
@@ -125,71 +146,72 @@
         return total
 
     line_copies = []
-    for k in far_first:
+    for k, near in zip(far_first, reversed(far_first)):
         line_send[k - 1] = plane_sum(k).astype(jnp.bfloat16)
         line_copies.append((k, remote(line_send.at[k - 1], line_recv.at[k - 1], line_peer(k))))
 
+        for copy in early_line[near]:
+            copy.wait_recv()
+        early_spread(flipped(z, near))
+    early_pair = {0: [share(table.at[core, xy], partner) for table in early]}
+
     grad = plane_sum(0)
-    for copy in small_loads:
-        copy.wait()
-    step = jnp.full((8, LANES), step_ref[0], jnp.int32)
-    first_scale = 1.0 - power(BETA1, step)
-    second_scale = 1.0 - power(BETA2, step)
-
-    for copy in master_line:
-        copy.wait_recv()
-    column = masters.at[core, xy]
-    master_plane = [(p, share(column, plane_peer(p))) for p in diagonal_first]
-    master_pair = [share(column, partner)]
-
     for k, copy in line_copies:
         copy.wait_recv()
         grad = grad + line_recv[k - 1].astype(jnp.float32)
     grad = grad / jnp.float32(count)
     new_m1 = 0.9 * m1[...] + 0.1 * grad
     new_m2 = 0.999 * m2[...] + 0.001 * grad * grad
-    update = (new_m1 / first_scale) / (jnp.sqrt(new_m2 / second_scale) + 1e-06)
-    updates[core, xy, z] = update + 0.1 * masters[core, xy, z]
-    m1_new[...] = new_m1
-    m2_new[...] = new_m2
-
-    update_line = [(k, share(updates.at[core, xy, z], line_peer(k))) for k in far_first]
+    update = update_of(new_m1, new_m2, masters[core, xy, z])
+    deltas[core, xy, z] = (update - guess.astype(jnp.float32)).astype(jnp.bfloat16)
+    update_line = [(k, share(deltas.at[core, xy, z], line_peer(k))) for k in far_first]
     update_plane, update_pair = [], []
 
     def spread(at_z):
-        row = updates.at[core, xy, at_z]
+        row = deltas.at[core, xy, at_z]
         for p in diagonal_first:
             update_plane.append((p, at_z, share(row, plane_peer(p))))
         update_pair.append((xy, at_z, share(row, partner)))
 
-    def square_sum(table, sums, side, at, j):
-        values = table[side, at, j]
+    def put_sum(sums, values, side, at, j):
         sums[(side * plane + at) * line + j] = jnp.sum(values * values, axis=0)
 
-    def square_sums(table, sums, side, at):
+    def weight_sums(side, at):
         for j in range(line):
-            square_sum(table, sums, side, at, j)
+            put_sum(wsums, masters[side, at, j], side, at, j)
+
+    def update_sum(side, at, j):
+        values = guesses[side, at, j].astype(jnp.float32) + deltas[side, at, j].astype(jnp.float32)
+        put_sum(usums, values, side, at, j)
 
     spread(z)
-    square_sums(masters, wsums, core, xy)
-    for p, copy in master_plane:
+    mine[...] = update
+    m1_new[...] = new_m1
+    m2_new[...] = new_m2
+    weight_sums(core, xy)
+    for turn, (k, copy) in enumerate(reversed(update_line)):
+        copy.wait_recv()
+        spread(flipped(z, k))
+        if turn == line - 3:
+            for p in diagonal_first:
+                for early_copy in early_plane[p]:
+                    early_copy.wait_recv()
+                at = flipped(xy, p)
+                early_pair[p] = [share(table.at[core, at], partner) for table in early]
+                weight_sums(core, at)
+    for j in range(line):
+        update_sum(core, xy, j)
+    for p, at_z, copy in update_plane:
         copy.wait_recv()
         at = flipped(xy, p)
-        master_pair.append(share(masters.at[core, at], partner))
-        square_sums(masters, wsums, core, at)
-    for k, copy in reversed(update_line):
-        copy.wait_recv()
-        spread(flipped(z, k))
-    square_sums(updates, usums, core, xy)
-    for p, at_z, copy in update_plane:
-        copy.wait_recv()
-        at = flipped(xy, p)
-        update_pair.append((at, at_z, share(updates.at[core, at, at_z], partner)))
-        square_sum(updates, usums, core, at, at_z)
-
-    for p, copy in zip([0] + diagonal_first, master_pair):
-        copy.wait_recv()
-        square_sums(masters, wsums, other, flipped(xy, p))
+        update_pair.append((at, at_z, share(deltas.at[core, at, at_z], partner)))
+        update_sum(core, at, at_z)
+
+    for p in [0] + diagonal_first:
+        for copy in early_pair[p]:
+            copy.wait_recv()
+        weight_sums(other, flipped(xy, p))
+    rows_load.wait()
 
     index0 = lax.broadcasted_iota(jnp.int32, (count, count), 0)
     index1 = lax.broadcasted_iota(jnp.int32, (count, count), 1)
@@ -213,7 +235,7 @@
 
     for at, at_z, copy in update_pair:
         copy.wait_recv()
-        square_sum(updates, usums, other, at, at_z)
+        update_sum(other, at, at_z)
 
     ratio = jnp.sqrt(wsq / (over_tensor(usums) + 1e-06))
     column = jnp.sum(jnp.where(index0 == index1, ratio, 0.0), axis=1, keepdims=True)
@@ -224,7 +246,7 @@
 
 def finish(
     line, plane,
-    masters, updates, ratios, m1_new, m2_new,
+    masters, guesses, deltas, ratios, m1_new, m2_new, mine,
     weights_out, master_out, moment1_out, moment2_out,
     weights, master_new, sem,
 ):
@@ -236,11 +258,11 @@
     for copy in copies:
         copy.start()
 
-    def new_row(side, at, j):
-        scale = ratios[pl.ds((side * plane + at) * line + j, 1), :]
-        return masters[side, at, j] - scale * updates[side, at, j]
-
-    master_new[...] = new_row(me % 2, me // 2 % plane, me // (2 * plane))
+    def scale(side, at, j):
+        return ratios[pl.ds((side * plane + at) * line + j, 1), :]
+
+    place = (me % 2, me // 2 % plane, me // (2 * plane))
+    master_new[...] = masters[place] - scale(*place) * mine[...]
     copies.append(pltpu.make_async_copy(master_new, master_out, sem.at[2]))
     copies[-1].start()
 
@@ -248,7 +270,9 @@
     def _(j):
         for at in range(plane):
             for side in range(2):
-                weights[j, at, side] = new_row(side, at, j).astype(jnp.bfloat16)
+                update = guesses[side, at, j].astype(jnp.float32) + deltas[side, at, j].astype(jnp.float32)
+                new_row = masters[side, at, j] - scale(side, at, j) * update
+                weights[j, at, side] = new_row.astype(jnp.bfloat16)
         pltpu.make_async_copy(weights.at[j], weights_out.at[j], sem.at[3 + j]).start()
 
     for j in range(line):
@@ -269,19 +293,21 @@
     hbm = pl.BlockSpec(memory_space=pltpu.HBM)
     vmem = pl.BlockSpec(memory_space=pltpu.VMEM)
     table = (2, plane, line) + row
-    remotes = line + line * (plane - 1) + 2 * (line - 1) + plane - 1 + plane
-    remotes += line - 1 + line * (plane - 1) + line * plane
+    gathered = line - 1 + line * (plane - 1)
+    remotes = line + gathered + 2 * gathered + 2 * plane + gathered + line * plane
     state = pl.pallas_call(
         functools.partial(kernel, count, line, plane),
         out_shape=(
             jax.ShapeDtypeStruct(table, f32),
-            jax.ShapeDtypeStruct(table, f32),
+            jax.ShapeDtypeStruct(table, bf16),
+            jax.ShapeDtypeStruct(table, bf16),
             jax.ShapeDtypeStruct((count, LANES), f32),
+            jax.ShapeDtypeStruct(row, f32),
             jax.ShapeDtypeStruct(row, f32),
             jax.ShapeDtypeStruct(row, f32),
         ),
         in_specs=[hbm] * 5 + [pl.BlockSpec(memory_space=pltpu.SMEM)],
-        out_specs=(vmem,) * 5,
+        out_specs=(vmem,) * 7,
         scratch_shapes=[
             pltpu.VMEM((line, plane) + row, f32),
             pltpu.VMEM((line, plane) + row, f32),
@@ -317,7 +343,7 @@
             jax.ShapeDtypeStruct(row, f32),
             jax.ShapeDtypeStruct(row, f32),
         ),
-        in_specs=[vmem] * 5,
+        in_specs=[vmem] * 7,
         out_specs=(hbm,) * 4,
         scratch_shapes=[
             pltpu.VMEM((line, plane, 2) + row, bf16),

time: 25.2 us -> 25.2 us (level)
  no operation moved by 1% of the time
where the time goes in v3:
time: 25.2 us; the launch traced here: 25.1 us
  Pallas kernels  23.8 us (94%)
  between operations  1.29 us (5%)
    pallas_call x1, Pallas kernels, body(): pl.pallas_call(functools.partial(kernel, count, line, plane), out_shape=(...  22.9 us
    pallas_call x1, Pallas kernels, body(): pl.pallas_call(functools.partial(finish, line, plane), out_shape=(jax.Sha...  0.89 us

profile of v3, /device:TPU:1, one launch (start us, length us, event | category | flops | bytes accessed | tf_op | source)
XLA Modules:
  0.0 25.1 jit_solution(14271263986030699787)
XLA Ops:
  1.3 22.9 %exchange.1 = (f32[2,4,4,5,8,128]{5,4,3,2,1,0:T(8,128)S(1)}, bf16[2,4,4,5,8,128]{5,4,3,2,1,0:T(8,128)(2,1)S(1)}, bf16[2,4,4,5,8,128]{5,4,3,2,1,0:T(8,128)(2,1)S(...) custom-call(f32[4,4,2,5,8,128]{5,4,3,2,1,0:T(8,128)} %bitcast.8, ...), custom_call_target="tpu_custom_call" | custom-call | tf_op jit(solution)/shard_map/exchange/pallas_call | solution.py:298
  24.2 0.9 %finish.1 = (bf16[4,4,2,5,8,128]{5,4,3,2,1,0:T(8,128)(2,1)}, f32[5,8,128]{2,1,0:T(8,128)}, f32[5,8,128]{2,1,0:T(8,128)}, f32[5,8,128]{2,1,0:T(8,128)}) custom-call(f32[2,4,4,5,8,128]{5,4,3,2,1,0:T(8,128)S(1)} %get-tuple-element.15.masters, bf16[2,4,4,5,8,128]{5,4,3,2,1,0:T(8,128)(2,1)S(1)} %get-tuple-element.16.guesses, ...), custom_call_target="tpu_custom_call" | custom-call | tf_op jit(solution)/shard_map/finish/pallas_call | solution.py:338

commit v4 on v3

--- a/solution.py
+++ b/solution.py
@@ -126,7 +126,6 @@
 
     for k in far_first:
         early_line[k].append(share(guesses.at[core, xy, z], line_peer(k)))
-    early_spread(z)
 
     plane_copies = {}
     for k, load, copy in zip(layers, our_loads, pair_copies):
@@ -137,6 +136,8 @@
             chip = ours[k, at] + pair_recv[k, at].astype(jnp.float32)
             plane_send[k, p - 1] = chip.astype(jnp.bfloat16)
             plane_copies[k, p] = remote(plane_send.at[k, p - 1], plane_recv.at[k, p - 1], plane_peer(p))
+
+    early_spread(z)
 
     def plane_sum(k):
         total = ours[k, xy] + pair_recv[k, xy].astype(jnp.float32)

time: 25.2 us -> 24.6 us (0.976)
  Pallas kernels: 23.8 us -> 23.2 us
    pallas_call x1, Pallas kernels: 22.9 us -> 22.3 us  [body(): pl.pallas_call(functools.partial(kernel, count, line, plane), out_shape=(...]
where the time goes in v4:
time: 24.6 us; the launch traced here: 24.5 us
  Pallas kernels  23.2 us (94%)
  between operations  1.29 us (5%)
    pallas_call x1, Pallas kernels, body(): pl.pallas_call(functools.partial(kernel, count, line, plane), out_shape=(...  22.3 us
    pallas_call x1, Pallas kernels, body(): pl.pallas_call(functools.partial(finish, line, plane), out_shape=(jax.Sha...  0.89 us

profile of v4, /device:TPU:1, one launch (start us, length us, event | category | flops | bytes accessed | tf_op | source)
XLA Modules:
  0.0 24.5 jit_solution(665410321061929484)
XLA Ops:
  1.3 22.3 %exchange.1 = (f32[2,4,4,5,8,128]{5,4,3,2,1,0:T(8,128)S(1)}, bf16[2,4,4,5,8,128]{5,4,3,2,1,0:T(8,128)(2,1)S(1)}, bf16[2,4,4,5,8,128]{5,4,3,2,1,0:T(8,128)(2,1)S(...) custom-call(f32[4,4,2,5,8,128]{5,4,3,2,1,0:T(8,128)} %bitcast.8, ...), custom_call_target="tpu_custom_call" | custom-call | tf_op jit(solution)/shard_map/exchange/pallas_call | solution.py:299
  23.6 0.9 %finish.1 = (bf16[4,4,2,5,8,128]{5,4,3,2,1,0:T(8,128)(2,1)}, f32[5,8,128]{2,1,0:T(8,128)}, f32[5,8,128]{2,1,0:T(8,128)}, f32[5,8,128]{2,1,0:T(8,128)}) custom-call(f32[2,4,4,5,8,128]{5,4,3,2,1,0:T(8,128)S(1)} %get-tuple-element.15.masters, bf16[2,4,4,5,8,128]{5,4,3,2,1,0:T(8,128)(2,1)S(1)} %get-tuple-element.16.guesses, ...), custom_call_target="tpu_custom_call" | custom-call | tf_op jit(solution)/shard_map/finish/pallas_call | solution.py:339
